TPU v7x, 32 devices: a whole 2x2x4 slice. The times are simulated.
32 devices in a mesh: expert: 16 (over z, y, core), token: 2 (over x).
Axes of the slice: x: 2, y: 2, z: 4, core: 2. Of those that a mesh axis runs over, the one named last changes fastest.
Arguments:
- cotangent: bfloat16 [4096, 2048], P(('expert', 'token')), may hold values from -6 to 6
- expert_ids: int32 [4096, 6], P(('expert', 'token')), may hold values from 0 to 15, all different within a row; in each aligned block of 128 rows (0 to 127, 128 to 255, ...) at most 56 rows name the same one
- gate_values: float32 [4096, 6], P(('expert', 'token')), may hold values from 0.05 to 0.45
- hidden_pre: bfloat16 [16, 1792, 768], P('expert', 'token'), may hold values from -8 to 8
- up_weight: bfloat16 [16, 2048, 768], P('expert'), may hold values from -0.125 to 0.125
- down_weight: bfloat16 [16, 2048, 768], P('expert'), may hold values from -0.21875 to 0.21875
Outputs:
- input_grad: bfloat16 [4096, 2048], P(('expert', 'token'))
- down_grad: bfloat16 [16, 2048, 768], P('expert', 'token')
Inputs may be any that keep to these rules, and one draw needn't show every extreme that they name: `expert_ids`: each row names 6 different experts. Among the 128 rows of one device no expert is named more than 56 times, and in every draw some expert is named exactly 56 times by the rows of some device.
All inputs are finite; a program needn't handle non-finite values.
Results may differ from a plain program's by a relative error of at most 0.007.
Values may be sent and summed in bfloat16 or wider, within the bound.
A program may use at most 128 MiB of HBM per device.

v0:
```python
import jax
import jax.numpy as jnp
from jax import lax
from jax.sharding import PartitionSpec as P

grad_scale = 0.03125
root_half = 0.7071067811865476
inv_root_two_pi = 0.3989422804014327


def slope_and_act(hidden_rows):
    values = hidden_rows.astype(jnp.float32)
    normal_cdf = 0.5 * (1.0 + lax.erf(values * root_half))
    density = inv_root_two_pi * jnp.exp(-0.5 * values * values)
    slopes = normal_cdf + values * density
    active = (values * normal_cdf).astype(jnp.bfloat16)
    return (slopes, active)


def route_tables(expert_ids, experts, capacity):
    routes = expert_ids.reshape(-1)
    one_hot = (routes[:, None] == jnp.arange(experts, dtype=jnp.int32)[None, :]).astype(jnp.int32)
    earlier = jnp.cumsum(one_hot, axis=0) - one_hot
    rank_in = jnp.sum(earlier * one_hot, axis=1)
    target = routes * capacity + rank_in
    slot_match = target[None, :] == jnp.arange(experts * capacity, dtype=jnp.int32)[:, None]
    route_index = jnp.arange(routes.shape[0], dtype=jnp.int32)[None, :]
    route_of_slot = jnp.sum(jnp.where(slot_match, route_index, 0), axis=1)
    slot_live = jnp.any(slot_match, axis=1)
    return (target, route_of_slot, slot_live)


def dispatch(slot_rows, experts):
    shaped = slot_rows.reshape(experts, -1, slot_rows.shape[1])
    arrived = lax.all_to_all(shaped, "expert", split_axis=0, concat_axis=0, tiled=True)
    return arrived.reshape(slot_rows.shape)


def transpose_jacobian(token_rows, tables, slopes, up_weight, down_weight, gate_values, experts):
    target, route_of_slot, slot_live = tables
    top_count = gate_values.shape[1]
    picked = jnp.take(token_rows, route_of_slot // top_count, axis=0)
    picked = jnp.where(slot_live[:, None], picked, jnp.zeros_like(picked))
    arrived = dispatch(picked, experts)
    inner_prod = jnp.dot(arrived, down_weight, preferred_element_type=jnp.float32)
    scaled = (inner_prod * slopes).astype(jnp.bfloat16)
    pieces = lax.dot_general(
        scaled, up_weight, (((1,), (1,)), ((), ())), preferred_element_type=jnp.float32
    ).astype(jnp.bfloat16)
    shaped = pieces.reshape(experts, -1, pieces.shape[1])
    returned = lax.all_to_all(shaped, "expert", split_axis=0, concat_axis=0, tiled=True).reshape(
        pieces.shape
    )
    per_route = jnp.take(returned, target, axis=0).astype(jnp.float32)
    per_route = per_route.reshape(gate_values.shape[0], top_count, -1)
    combined = jnp.sum(per_route * gate_values[:, :, None], axis=1)
    return combined.astype(jnp.bfloat16)


def body(cotangent, expert_ids, gate_values, hidden_pre, up_weight, down_weight):
    experts = lax.axis_size("expert")
    slopes, active = slope_and_act(hidden_pre[0])
    capacity = slopes.shape[0] // experts
    tables = route_tables(expert_ids, experts, capacity)
    first_term = transpose_jacobian(
        cotangent, tables, slopes, up_weight[0], down_weight[0], gate_values, experts
    )
    second = transpose_jacobian(
        first_term, tables, slopes, up_weight[0], down_weight[0], gate_values, experts
    )
    input_grad = (
        cotangent.astype(jnp.float32) + first_term.astype(jnp.float32) + second.astype(jnp.float32)
    ).astype(jnp.bfloat16)
    target, route_of_slot, slot_live = tables
    top_count = gate_values.shape[1]
    slot_gate = jnp.where(slot_live, jnp.take(gate_values.reshape(-1), route_of_slot), 0.0)
    picked = jnp.take(input_grad, route_of_slot // top_count, axis=0).astype(jnp.float32)
    routed = (picked * slot_gate[:, None]).astype(jnp.bfloat16)
    arrived = dispatch(routed, experts)
    grad_parts = lax.all_to_all(arrived, "token", split_axis=1, concat_axis=0, tiled=True)
    summed = lax.dot_general(
        grad_parts,
        lax.all_gather(active, "token", axis=0, tiled=True),
        (((0,), (0,)), ((), ())),
        preferred_element_type=jnp.float32,
    )
    grad_out = (summed * grad_scale).astype(jnp.bfloat16)[None]
    return (input_grad, grad_out)


def solution(mesh):
    in_specs = (
        P(("expert", "token"), None),
        P(("expert", "token"), None),
        P(("expert", "token"), None),
        P("expert", "token", None),
        P("expert", None, None),
        P("expert", None, None),
    )
    out_specs = (P(("expert", "token"), None), P("expert", "token", None))
    return jax.shard_map(body, mesh=mesh, in_specs=in_specs, out_specs=out_specs, check_vma=False)
```

profile of v0, /device:TPU:0, one launch (start us, length us, event | category | flops | bytes accessed | tf_op | source)
XLA Modules:
  0.0 619.0 jit_solution(13457145134131405697)
XLA Ops:
  11.3 9.9 %gather_fusion.1 = bf16[896,2048]{1,0:T(8,128)(2,1)} fusion(bf16[128,2048]{1,0:T(8,128)(2,1)} %param.10, s32[1024]{0:T(1024)S(1)} %pad_clamp_fusion.2), kind=kCustom, calls=%fused_computation.clone | custom fusion | bytes 7343616 | tf_op jit(solution)/shard_map/jit(_take)/gather | solution.py:42
  23.7 88.2 %all_to_all.44 = bf16[16,56,2048]{2,1,0:T(8,128)(2,1)} all-to-all(bf16[16,56,2048]{2,1,0:T(8,128)(2,1)S(1)} %bitcast.78), channel_id=1, replica_groups=mesh['expert'=16,'token'=2] {'expert'}, dimensions={0} | all-to-all | bytes 7340032 | tf_op jit(solution)/shard_map/all_to_all | solution.py:35
  111.9 11.0 %convolution_convert_fusion.1 = bf16[896,2048]{1,0:T(8,128)(2,1)} fusion(bf16[1,2048,768]{2,1,0:T(8,128)(2,1)S(1)} %copy-done, bf16[896,2048]{1,0:T(8,128)(2,1)} %bitcast.82, bf16[1,2048,768]{2,1,0:T(8,128)(2,1)} %param.15, bf16[1,896,768]{2,1,0:T(8,128)(2,1)} %param.13), kind=kOutput, calls=%fused_computation.17 | convolution fusion | flops 5646548992 | bytes 15007744 | tf_op jit(solution)/shard_map/dot_general | solution.py:47
  122.9 5.4 all-to-all-start.1
  128.5 68.3 %all-to-all-done.1 = bf16[16,56,2048]{2,1,0:T(8,128)(2,1)} async-done(((bf16[16,56,2048]{2,1,0:T(8,128)(2,1)}), bf16[16,56,2048]{2,1,0:T(8,128)(2,1)}, u32[]{:S(2)}, u32[]{:S(2)}) %all-to-all-start.1) | async-done | bytes 3670048 | tf_op jit(solution)/shard_map/all_to_all | solution.py:51
  196.8 9.6 %gather_fusion.2 = bf16[768,2048]{1,0:T(8,128)(2,1)} fusion(bf16[896,2048]{1,0:T(8,128)(2,1)} %bitcast.8, s32[1024]{0:T(1024)S(1)} %pad_clamp_fusion.1), kind=kCustom, calls=%fused_computation.1.clone | custom fusion | bytes 6294528 | tf_op jit(solution)/shard_map/jit(_take)/gather | solution.py:54
  206.4 5.1 select_convert_fusion.1
  211.5 7.8 %reshape.140 = f32[128,6,2048]{2,1,0:T(8,128)} reshape(f32[768,2048]{1,0:T(8,128)} %select_convert_fusion.1) | data formatting | bytes 12582912 | tf_op jit(solution)/shard_map/reshape | solution.py:55
  219.3 7.4 %multiply_reduce_fusion.1 = bf16[128,2048]{1,0:T(8,128)(2,1)} fusion(f32[128,6,2048]{2,1,0:T(8,128)} %reshape.140, f32[128,6]{1,0:T(8,128)S(1)} %copy.29), kind=kLoop, calls=%fused_computation.7 | loop fusion | flops 2883584 | bytes 6818816 | tf_op jit(solution)/shard_map/reduce_sum | solution.py:56
  226.7 9.9 %gather_fusion.3 = bf16[896,2048]{1,0:T(8,128)(2,1)} fusion(bf16[128,2048]{1,0:T(8,128)(2,1)} %multiply_reduce_fusion.1, s32[1024]{0:T(1024)S(1)} %pad_clamp_fusion.2), kind=kCustom, calls=%fused_computation.2.clone | custom fusion | bytes 7343616 | tf_op jit(solution)/shard_map/jit(_take)/gather | solution.py:42
  239.1 98.3 %all_to_all.45 = bf16[16,56,2048]{2,1,0:T(8,128)(2,1)} all-to-all(bf16[16,56,2048]{2,1,0:T(8,128)(2,1)S(1)} %bitcast.79), channel_id=1, replica_groups=mesh['expert'=16,'token'=2] {'expert'}, dimensions={0} | all-to-all | bytes 7340032 | tf_op jit(solution)/shard_map/all_to_all | solution.py:35
  337.4 11.0 %convolution_convert_fusion = bf16[896,2048]{1,0:T(8,128)(2,1)} fusion(bf16[1,2048,768]{2,1,0:T(8,128)(2,1)S(1)} %copy-done, bf16[896,2048]{1,0:T(8,128)(2,1)} %bitcast.83, bf16[1,2048,768]{2,1,0:T(8,128)(2,1)} %param.15, bf16[1,896,768]{2,1,0:T(8,128)(2,1)} %param.13), kind=kOutput, calls=%fused_computation.16 | convolution fusion | flops 5646548992 | bytes 15007744 | tf_op jit(solution)/shard_map/dot_general | solution.py:47
  348.4 5.3 all-to-all-start.3
  357.6 64.6 %all-to-all-done.3 = bf16[16,56,2048]{2,1,0:T(8,128)(2,1)} async-done(((bf16[16,56,2048]{2,1,0:T(8,128)(2,1)}), bf16[16,56,2048]{2,1,0:T(8,128)(2,1)}, u32[]{:S(2)}, u32[]{:S(2)}) %all-to-all-start.3) | async-done | bytes 3670048 | tf_op jit(solution)/shard_map/all_to_all | solution.py:51
  422.1 8.8 %gather_fusion.4 = bf16[768,2048]{1,0:T(8,128)(2,1)S(1)} fusion(bf16[896,2048]{1,0:T(8,128)(2,1)} %bitcast.12, s32[1024]{0:T(1024)S(1)} %pad_clamp_fusion.1), kind=kCustom, calls=%fused_computation.4.clone | custom fusion | bytes 6294528 | tf_op jit(solution)/shard_map/jit(_take)/gather | solution.py:54
  434.2 7.8 %reshape.142 = f32[128,6,2048]{2,1,0:T(8,128)} reshape(f32[768,2048]{1,0:T(8,128)} %select_convert_fusion) | data formatting | bytes 12582912 | tf_op jit(solution)/shard_map/reshape | solution.py:55
  442.0 6.7 %multiply_reduce_fusion = bf16[128,2048]{1,0:T(8,128)(2,1)S(1)} fusion(f32[128,6,2048]{2,1,0:T(8,128)} %reshape.142, f32[128,6]{1,0:T(8,128)S(1)} %copy.29), kind=kLoop, calls=%fused_computation.6 | loop fusion | flops 2883584 | bytes 6818816 | tf_op jit(solution)/shard_map/reduce_sum | solution.py:56
  457.9 17.7 %all-to-all-start.4 = ((bf16[16,56,2048]{2,1,0:T(8,128)(2,1)}), bf16[16,56,2048]{2,1,0:T(8,128)(2,1)}, u32[]{:S(2)}, u32[]{:S(2)}) async-start(bf16[16,56,2048]{2,1,0:T(8,128)(2,1)} %bitcast.77), calls=%async_computation.4 | async-start | bytes 7340032 | tf_op jit(solution)/shard_map/all_to_all | solution.py:35
  477.2 66.8 %all-to-all-done.4 = bf16[16,56,2048]{2,1,0:T(8,128)(2,1)} async-done(((bf16[16,56,2048]{2,1,0:T(8,128)(2,1)}), bf16[16,56,2048]{2,1,0:T(8,128)(2,1)}, u32[]{:S(2)}, u32[]{:S(2)}) %all-to-all-start.4) | async-done | bytes 3670048 | tf_op jit(solution)/shard_map/all_to_all | solution.py:35
  544.0 7.2 %all_to_all.34 = bf16[896,2,1024]{2,1,0:T(2,128)(2,1)} reshape(bf16[16,56,2048]{2,1,0:T(8,128)(2,1)} %all-to-all-done.4) | data formatting | bytes 7340032 | tf_op jit(solution)/shard_map/all_to_all | solution.py:80
  551.2 5.1 copy.31
  556.3 5.4 all-to-all-start.5
  561.7 43.2 %all-to-all-done.5 = bf16[896,2,1024]{2,0,1:T(8,128)(2,1)} async-done(((bf16[896,2,1024]{2,0,1:T(8,128)(2,1)}), bf16[896,2,1024]{2,0,1:T(8,128)(2,1)}, u32[]{:S(2)}, u32[]{:S(2)}) %all-to-all-start.5) | async-done | bytes 3670048 | tf_op jit(solution)/shard_map/all_to_all | solution.py:80
  604.9 7.3 %fusion.18 = bf16[1,1024,768]{2,1,0:T(8,128)(2,1)} fusion(bf16[1792,1024]{1,0:T(8,128)(2,1)} %bitcast.15, bf16[1792,768]{1,0:T(8,128)(2,1)} %all-gather.2.cloned.1.call-done), kind=kOutput, calls=%fused_computation.39 | convolution fusion | flops 2820145152 | bytes 7995392 | tf_op jit(solution)/shard_map/dot_general | solution.py:81
  (45 shorter events, 27.0 us)
Async XLA Ops:
  7.2 104.7 %copy-start = (bf16[1,2048,768]{2,1,0:T(8,128)(2,1)S(1)}, bf16[1,2048,768]{2,1,0:T(8,128)(2,1)}, u32[]{:S(2)}) copy-start(bf16[1,2048,768]{2,1,0:T(8,128)(2,1)} %param.14) | copy-start | bytes 9437188
  122.9 5.5 copy-start.6
  122.9 73.9 %all-to-all-start.1 = ((bf16[16,56,2048]{2,1,0:T(8,128)(2,1)}), bf16[16,56,2048]{2,1,0:T(8,128)(2,1)}, u32[]{:S(2)}, u32[]{:S(2)}) async-start(bf16[16,56,2048]{2,1,0:T(8,128)(2,1)} %bitcast.81), calls=%async_computation.1 | async-start | bytes 7340032 | tf_op jit(solution)/shard_map/all_to_all | solution.py:51
  348.4 73.7 %all-to-all-start.3 = ((bf16[16,56,2048]{2,1,0:T(8,128)(2,1)}), bf16[16,56,2048]{2,1,0:T(8,128)(2,1)}, u32[]{:S(2)}, u32[]{:S(2)}) async-start(bf16[16,56,2048]{2,1,0:T(8,128)(2,1)} %bitcast.80), calls=%async_computation.3 | async-start | bytes 7340032 | tf_op jit(solution)/shard_map/all_to_all | solution.py:51
  442.0 6.7 %copy-start.2 = (bf16[128,2048]{1,0:T(8,128)(2,1)S(1)}, bf16[128,2048]{1,0:T(8,128)(2,1)}, u32[]{:S(2)}) copy-start(bf16[128,2048]{1,0:T(8,128)(2,1)} %multiply_reduce_fusion.1) | copy-start | bytes 1572868
  442.0 6.7 %copy-start.3 = (bf16[128,2048]{1,0:T(8,128)(2,1)S(1)}, bf16[128,2048]{1,0:T(8,128)(2,1)}, u32[]{:S(2)}) copy-start(bf16[128,2048]{1,0:T(8,128)(2,1)} %param.10) | copy-start | bytes 1572868
  449.0 5.0 copy-start.4
  457.9 17.8 %copy-start.5 = (bf16[1,896,768]{2,1,0:T(8,128)(2,1)S(1)}, bf16[1,896,768]{2,1,0:T(8,128)(2,1)}, u32[]{:S(2)}) copy-start(bf16[1,896,768]{2,1,0:T(8,128)(2,1)} %param.13) | copy-start | bytes 4128772
  457.9 86.1 %all-to-all-start.4 = ((bf16[16,56,2048]{2,1,0:T(8,128)(2,1)}), bf16[16,56,2048]{2,1,0:T(8,128)(2,1)}, u32[]{:S(2)}, u32[]{:S(2)}) async-start(bf16[16,56,2048]{2,1,0:T(8,128)(2,1)} %bitcast.77), calls=%async_computation.4 | async-start | bytes 7340032 | tf_op jit(solution)/shard_map/all_to_all | solution.py:35
  475.6 86.1 %all-gather.2.cloned.1.call-start = ((), (), s32[]{:S(2)}) async-start(), calls=%async_computation.6 | async-start | bytes 4128768 | tf_op jit(solution)/shard_map/all_gather | solution.py:83
  556.3 48.6 %all-to-all-start.5 = ((bf16[896,2,1024]{2,0,1:T(8,128)(2,1)}), bf16[896,2,1024]{2,0,1:T(8,128)(2,1)}, u32[]{:S(2)}, u32[]{:S(2)}) async-start(bf16[896,2,1024]{2,0,1:T(8,128)(2,1)} %copy.31), calls=%async_computation.5 | async-start | bytes 7340032 | tf_op jit(solution)/shard_map/all_to_all | solution.py:80
  604.9 7.3 %copy-start.1 = (bf16[1,2048,768]{2,1,0:T(8,128)(2,1)S(1)}, bf16[1,2048,768]{2,1,0:T(8,128)(2,1)}, u32[]{:S(2)}) copy-start(bf16[1,2048,768]{2,1,0:T(8,128)(2,1)} %param.14) | copy-start | bytes 9437188
Sparse Core Ops, SparseCore 0:
  478.5 41.7 all-gather.1
where the time goes:
time: 631 us; the launch traced here: 619 us
  waiting for transfers between devices  243 us (39%)
  blocking collectives  186 us (29%)
  local copies, waits for them, and re-layouts  76.6 us (12%)
  other arithmetic  35.7 us (6%)
  starting transfers between devices  33.9 us (5%)
  matrix products  29.2 us (5%)
  between operations  14.3 us (2%)
    all_to_all x2, blocking collectives, dispatch(): lax.all_to_all(shaped, 'expert', split_axis=0, concat_axis=0, tiled=True)  186 us
    all_to_all x2, waiting for transfers between devices, transpose_jacobian(): lax.all_to_all(shaped, 'expert', split_axis=0, concat_axis=0, tiled=True)  133 us
    all_to_all x1, waiting for transfers between devices, dispatch(): lax.all_to_all(shaped, 'expert', split_axis=0, concat_axis=0, tiled=True)  66.8 us
    all_to_all x1, waiting for transfers between devices, body(): lax.all_to_all(arrived, 'token', split_axis=1, concat_axis=0, tiled=True)  43.2 us
    dot_general x2, matrix products, transpose_jacobian(): lax.dot_general(scaled, up_weight, (((1,), (1,)), ((), ())), preferred_el...  22 us
    gather x2, local copies, waits for them, and re-layouts, transpose_jacobian(): picked = jnp.take(token_rows, route_of_slot // top_count, axis=0)  19.8 us
    gather x2, local copies, waits for them, and re-layouts, transpose_jacobian(): per_route = jnp.take(returned, target, axis=0).astype(jnp.float32)  18.5 us
    all_to_all x1, starting transfers between devices, dispatch(): lax.all_to_all(shaped, 'expert', split_axis=0, concat_axis=0, tiled=True)  17.7 us
  transfers between devices with their start and end apart: 5, of which 4 were waited for; matrix products, arithmetic and copies ran while one was open for 2% of the time, Pallas kernels for 0%

commit v1 on v0

v1 whole, which is shorter than its diff:
```python
import jax
import jax.numpy as jnp
from jax import lax
from jax.sharding import PartitionSpec as P

grad_scale = 0.03125
root_half = 0.7071067811865476
inv_root_two_pi = 0.3989422804014327


def slope_and_act(hidden_rows):
    values = hidden_rows.astype(jnp.float32)
    normal_cdf = 0.5 * (1.0 + lax.erf(values * root_half))
    density = inv_root_two_pi * jnp.exp(-0.5 * values * values)
    slopes = normal_cdf + values * density
    active = (values * normal_cdf).astype(jnp.bfloat16)
    return (slopes, active)


def slot_tables(ids, gates, capacity):
    me = lax.axis_index("expert")
    hit = ids == me
    match = jnp.any(hit, axis=2)
    gate = jnp.sum(jnp.where(hit, gates, 0.0), axis=2)
    rows = ids.shape[1]
    order = jnp.arange(rows, dtype=jnp.int32)
    before = (order[:, None] < order[None, :]).astype(jnp.bfloat16)
    rank = jnp.dot(match.astype(jnp.bfloat16), before, preferred_element_type=jnp.float32)
    rank = jnp.where(match, rank.astype(jnp.int32), -1)
    chosen = rank[:, None, :] == jnp.arange(capacity, dtype=jnp.int32)[None, :, None]
    slot_gate = jnp.sum(jnp.where(chosen, gate[:, None, :], 0.0), axis=2)
    return chosen.astype(jnp.bfloat16), slot_gate


def gather_rows(rows):
    return lax.all_gather(rows, "expert", axis=0, tiled=False)


def scatter_sum(blocks):
    return lax.psum_scatter(blocks, "expert", scatter_dimension=0, tiled=False)


def pick(sel, rows):
    return lax.dot_general(
        sel, rows, (((2,), (1,)), ((0,), (0,))), preferred_element_type=jnp.float32
    ).astype(jnp.bfloat16)


def transpose_jacobian(token_rows, sel, slot_gate, slopes, up_weight, down_weight):
    blocks, capacity, rows = sel.shape
    everyone = gather_rows(token_rows)
    picked = pick(sel, everyone).reshape(blocks * capacity, -1)
    inner_prod = jnp.dot(picked, down_weight, preferred_element_type=jnp.float32)
    scaled = (inner_prod * slopes).astype(jnp.bfloat16)
    pieces = lax.dot_general(
        scaled, up_weight, (((1,), (1,)), ((), ())), preferred_element_type=jnp.float32
    ).astype(jnp.bfloat16)
    weighted = (pieces.astype(jnp.float32) * slot_gate.reshape(-1, 1)).astype(jnp.bfloat16)
    spread = lax.dot_general(
        sel,
        weighted.reshape(blocks, capacity, -1),
        (((1,), (1,)), ((0,), (0,))),
        preferred_element_type=jnp.float32,
    ).astype(jnp.bfloat16)
    return scatter_sum(spread)


def body(cotangent, expert_ids, gate_values, hidden_pre, up_weight, down_weight):
    experts = lax.axis_size("expert")
    groups = lax.axis_size("token")
    mine = lax.axis_index("token")
    slopes, active = slope_and_act(hidden_pre[0])
    capacity = slopes.shape[0] // experts
    both_ids = lax.all_gather(expert_ids, ("expert", "token"), axis=0, tiled=False)
    both_gates = lax.all_gather(gate_values, ("expert", "token"), axis=0, tiled=False)
    all_sel, all_gate = slot_tables(both_ids, both_gates, capacity)
    all_sel = all_sel.reshape(experts, groups, capacity, -1)
    all_gate = all_gate.reshape(experts, groups, capacity)
    sel = lax.dynamic_index_in_dim(all_sel, mine, 1, keepdims=False)
    slot_gate = lax.dynamic_index_in_dim(all_gate, mine, 1, keepdims=False)
    first_term = transpose_jacobian(
        cotangent, sel, slot_gate, slopes, up_weight[0], down_weight[0]
    )
    second = transpose_jacobian(
        first_term, sel, slot_gate, slopes, up_weight[0], down_weight[0]
    )
    input_grad = (
        cotangent.astype(jnp.float32) + first_term.astype(jnp.float32) + second.astype(jnp.float32)
    ).astype(jnp.bfloat16)
    rows = input_grad.shape[0]
    columns = lax.all_to_all(input_grad, "token", split_axis=1, concat_axis=0, tiled=True)
    everyone = gather_rows(columns).reshape(experts * groups, rows, -1)
    picked = pick(all_sel.reshape(experts * groups, capacity, rows), everyone)
    routed = (picked.astype(jnp.float32) * all_gate.reshape(-1, capacity, 1)).astype(jnp.bfloat16)
    acts = lax.all_gather(active, "token", axis=0, tiled=False)
    acts = acts.reshape(groups, experts, capacity, -1).transpose(1, 0, 2, 3)
    summed = lax.dot_general(
        routed.reshape(experts * groups * capacity, -1),
        acts.reshape(experts * groups * capacity, -1),
        (((0,), (0,)), ((), ())),
        preferred_element_type=jnp.float32,
    )
    grad_out = (summed * grad_scale).astype(jnp.bfloat16)[None]
    return (input_grad, grad_out)


def solution(mesh):
    in_specs = (
        P(("expert", "token"), None),
        P(("expert", "token"), None),
        P(("expert", "token"), None),
        P("expert", "token", None),
        P("expert", None, None),
        P("expert", None, None),
    )
    out_specs = (P(("expert", "token"), None), P("expert", "token", None))
    return jax.shard_map(body, mesh=mesh, in_specs=in_specs, out_specs=out_specs, check_vma=False)
```

time: 631 us -> 581 us (0.921); the launches traced: 619 us -> 580 us
  waiting for transfers between devices: 243 us -> 347 us
  local copies, waits for them, and re-layouts: 76.6 us -> 5.01 us
  blocking collectives: 186 us -> 149 us
  starting transfers between devices: 33.9 us -> 0.42 us
  other arithmetic: 35.7 us -> 3.31 us
  matrix products: 29.2 us -> 59.4 us
    all_to_all x4 -> x0, waiting for transfers between devices: 243 us -> none  [the longest x2 133 us: transpose_jacobian(): lax.all_to_all(shaped, 'expert', split_axis=0, concat_axis=0, tiled=True)]
    reduce_scatter x0 -> x2, waiting for transfers between devices: none -> 201 us  [scatter_sum(): return lax.psum_scatter(blocks, 'expert', scatter_dimension=0, tiled=False)]
    all_to_all x2 -> x1, blocking collectives: 186 us -> 11 us  [body(): lax.all_to_all(input_grad, 'token', split_axis=1, concat_axis=0, tiled=True)]
    all_gather x1 -> x4, waiting for transfers between devices: 0.02 us -> 146 us  [the longest x3 146 us: gather_rows(): return lax.all_gather(rows, 'expert', axis=0, tiled=False)]
    all_gather x0 -> x2, blocking collectives: none -> 138 us  [the longest x1 74 us: body(): lax.all_gather(expert_ids, ('expert', 'token'), axis=0, tiled=False)]
    gather x6 -> x0, local copies, waits for them, and re-layouts: 46.9 us -> none  [the longest x2 19.8 us: transpose_jacobian(): picked = jnp.take(token_rows, route_of_slot // top_count, axis=0)]
    all_to_all x4 -> x0, starting transfers between devices: 33.9 us -> none  [the longest x1 17.7 us: dispatch(): lax.all_to_all(shaped, 'expert', split_axis=0, concat_axis=0, tiled=True)]
    dot_general x1 -> x7, matrix products: 7.27 us -> 37.5 us  [the longest x3 17.6 us: pick(): lax.dot_general(sel, rows, (((2,), (1,)), ((0,), (0,))), preferred_elemen...]
  transfers between devices with their start and end apart: 5 -> 6, of which waited for: 4 -> 4; matrix products, arithmetic and copies ran while one was open for 2% -> 1% of each run, Pallas kernels for 0% -> 0%
where the time goes in v1:
time: 581 us; the launch traced here: 580 us
  waiting for transfers between devices  347 us (60%)
  blocking collectives  149 us (26%)
  matrix products  59.4 us (10%)
  between operations  15.4 us (3%)
    reduce_scatter x2, waiting for transfers between devices, scatter_sum(): return lax.psum_scatter(blocks, 'expert', scatter_dimension=0, tiled=False)  201 us
    all_gather x3, waiting for transfers between devices, gather_rows(): return lax.all_gather(rows, 'expert', axis=0, tiled=False)  146 us
    all_gather x1, blocking collectives, body(): lax.all_gather(expert_ids, ('expert', 'token'), axis=0, tiled=False)  74 us
    all_gather x1, blocking collectives, body(): lax.all_gather(gate_values, ('expert', 'token'), axis=0, tiled=False)  64.3 us
    dot_general x2, matrix products, transpose_jacobian(): lax.dot_general(scaled, up_weight, (((1,), (1,)), ((), ())), preferred_el...  21.9 us
    dot_general x3, matrix products, pick(): lax.dot_general(sel, rows, (((2,), (1,)), ((0,), (0,))), preferred_elemen...  17.6 us
    dot_general x2, matrix products, transpose_jacobian(): lax.dot_general(sel, weighted.reshape(blocks, capacity, -1), (((1,), (1,)...  15.5 us
  transfers between devices with their start and end apart: 6, of which 4 were waited for; matrix products, arithmetic and copies ran while one was open for 1% of the time, Pallas kernels for 0%

profile of v1, /device:TPU:0, one launch (start us, length us, event | category | flops | bytes accessed | tf_op | source)
XLA Modules:
  0.0 580.2 jit_solution(1380429993613920116)
XLA Ops:
  8.1 0.7 all-gather.14.cloned.1.call-update
  8.8 74.0 %all-gather = s32[4096,6]{0,1:T(8,128)S(1)} all-gather(s32[128,6]{0,1:T(8,128)} %param.7), channel_id=2, replica_groups=mesh['expert'=16,'token'=2] {'expert','token'}, dimensions={0}, use_global_device_ids=true | all-gather | bytes 101376 | tf_op jit(solution)/shard_map/all_gather | solution.py:74
  82.8 64.3 %all-gather.2 = f32[4096,6]{0,1:T(8,128)S(1)} all-gather(f32[128,6]{0,1:T(8,128)} %param.8), channel_id=4, replica_groups=mesh['expert'=16,'token'=2] {'expert','token'}, dimensions={0}, use_global_device_ids=true | all-gather | bytes 101376 | tf_op jit(solution)/shard_map/all_gather | solution.py:75
  147.2 0.1 fusion.25
  147.3 0.4 select_reduce_fusion
  147.8 0.1 mul.91
  147.9 6.4 %convolution_convert_fusion.3 = bf16[16,56,2048]{2,1,0:T(8,128)(2,1)} fusion(bf16[16,128,2048]{2,1,0:T(8,128)(2,1)} %bitcast.99, s32[16,1,128]{2,0,1:T(8,128)S(1)} %constant_dynamic-slice_fusion), kind=kOutput, calls=%fused_computation.13 | convolution fusion | flops 471711744 | bytes 12066816 | tf_op jit(solution)/shard_map/dot_general | solution.py:44
  154.4 11.0 %multiply_convert_fusion.2 = bf16[896,2048]{1,0:T(8,128)(2,1)} fusion(f32[896]{0:T(1024)S(1)} %mul.91, bf16[1,2048,768]{2,1,0:T(8,128)(2,1)S(1)} %copy-done, bf16[896,2048]{1,0:T(8,128)(2,1)} %bitcast.101, bf16[1,2048,768]{2,1,0:T(8,128)(2,1)} %param.11, bf16[1,896,768]{2,1,0:T(8,128)(2,1)} %param.9), kind=kOutput, calls=%fused_computation.2 | convolution fusion | flops 5652054016 | bytes 15011328 | tf_op jit(solution)/shard_map/dot_general | solution.py:55
  165.3 7.7 %convolution_convert_fusion.1 = bf16[16,128,2048]{2,1,0:T(8,128)(2,1)} fusion(bf16[16,56,2048]{2,1,0:T(8,128)(2,1)} %bitcast.105, s32[16,1,128]{2,0,1:T(8,128)S(1)} %constant_dynamic-slice_fusion), kind=kOutput, calls=%fused_computation.4 | convolution fusion | flops 474071040 | bytes 12066816 | tf_op jit(solution)/shard_map/dot_general | solution.py:59
  173.1 101.5 %reduce-scatter.3.cloned.1.call-done = bf16[1,128,2048]{2,1,0:T(8,128)(2,1)} async-done(((bf16[16,128,2048]{2,1,0:T(8,128)(2,1)}), bf16[1,128,2048]{2,1,0:T(8,128)(2,1)}) %reduce-scatter.3.cloned.1.call-update) | async-done | bytes 524304 | tf_op jit(solution)/shard_map/reduce_scatter | solution.py:40
  274.7 0.2 reduce-scatter.5.cloned.1.call-start
  274.9 75.9 %all-gather.8.cloned.1.call-done = bf16[16,128,2048]{2,1,0:T(8,128)(2,1)} async-done(((bf16[1,128,2048]{2,1,0:T(8,128)(2,1)}), bf16[16,128,2048]{2,1,0:T(8,128)(2,1)}) %all-gather.8.cloned.1.call-update) | async-done | bytes 8388624 | tf_op jit(solution)/shard_map/all_gather | solution.py:36
  350.8 6.4 %convolution_convert_fusion.2 = bf16[16,56,2048]{2,1,0:T(8,128)(2,1)} fusion(bf16[16,128,2048]{2,1,0:T(8,128)(2,1)} %all-gather.8.cloned.1.call-done, s32[16,1,128]{2,0,1:T(8,128)S(1)} %constant_dynamic-slice_fusion), kind=kOutput, calls=%fused_computation.12 | convolution fusion | flops 471711744 | bytes 12066816 | tf_op jit(solution)/shard_map/dot_general | solution.py:44
  357.2 11.0 %multiply_convert_fusion.1 = bf16[896,2048]{1,0:T(8,128)(2,1)} fusion(f32[896]{0:T(1024)S(1)} %mul.91, bf16[1,2048,768]{2,1,0:T(8,128)(2,1)S(1)} %copy-done, bf16[896,2048]{1,0:T(8,128)(2,1)} %bitcast.100, bf16[1,2048,768]{2,1,0:T(8,128)(2,1)} %param.11, bf16[1,896,768]{2,1,0:T(8,128)(2,1)} %param.9), kind=kOutput, calls=%fused_computation.1 | convolution fusion | flops 5652054016 | bytes 15011328 | tf_op jit(solution)/shard_map/dot_general | solution.py:55
  368.1 7.8 %convolution_convert_fusion = bf16[16,128,2048]{2,1,0:T(8,128)(2,1)} fusion(bf16[16,56,2048]{2,1,0:T(8,128)(2,1)} %bitcast.104, s32[16,1,128]{2,0,1:T(8,128)S(1)} %constant_dynamic-slice_fusion), kind=kOutput, calls=%fused_computation.3 | convolution fusion | flops 474071040 | bytes 12066816 | tf_op jit(solution)/shard_map/dot_general | solution.py:59
  376.0 1.2 copy-done.6
  377.3 1.5 fusion.19
  378.8 99.3 %reduce-scatter.5.cloned.1.call-done = bf16[1,128,2048]{2,1,0:T(8,128)(2,1)} async-done(((bf16[16,128,2048]{2,1,0:T(8,128)(2,1)}), bf16[1,128,2048]{2,1,0:T(8,128)(2,1)}) %reduce-scatter.5.cloned.1.call-update) | async-done | bytes 524304 | tf_op jit(solution)/shard_map/reduce_scatter | solution.py:40
  478.1 1.3 fusion.26
  479.5 11.0 %all_to_all.16 = bf16[128,2,1024]{2,0,1:T(8,128)(2,1)} all-to-all(bf16[128,2,1024]{2,0,1:T(8,128)(2,1)S(1)} %bitcast.109), channel_id=1, replica_groups=mesh['expert'=16,'token'=2] {'token'}, dimensions={1} | all-to-all | bytes 1048576 | tf_op jit(solution)/shard_map/all_to_all | solution.py:91
  490.5 3.6 copy.16
  494.1 69.9 %all-gather.10.cloned.1.call-done = bf16[16,256,1024]{2,1,0:T(8,128)(2,1)} async-done(((bf16[1,256,1024]{2,1,0:T(8,128)(2,1)}), bf16[16,256,1024]{2,1,0:T(8,128)(2,1)}) %all-gather.10.cloned.1.call-update) | async-done | bytes 8388624 | tf_op jit(solution)/shard_map/all_gather | solution.py:36
  564.0 4.8 multiply_convert_fusion
  568.8 4.3 fusion.24
  (31 shorter events, 0.6 us)
Async XLA Ops:
  8.0 146.4 %copy-start = (bf16[1,2048,768]{2,1,0:T(8,128)(2,1)S(1)}, bf16[1,2048,768]{2,1,0:T(8,128)(2,1)}, u32[]{:S(2)}) copy-start(bf16[1,2048,768]{2,1,0:T(8,128)(2,1)} %param.10) | copy-start | bytes 9437188
  8.0 139.9 %all-gather.14.cloned.1.call-start = ((), (), s32[]{:S(2)}) async-start(), calls=%async_computation.8 | async-start | bytes 8912896 | tf_op jit(solution)/shard_map/all_gather | solution.py:36
  8.7 265.9 %reduce-scatter.3.cloned.1.call-start = ((), (), s32[]{:S(2)}) async-start(), calls=%async_computation.3 | async-start | bytes 8912896 | tf_op jit(solution)/shard_map/reduce_scatter | solution.py:40
  173.1 177.7 %all-gather.8.cloned.1.call-start = ((), (), s32[]{:S(2)}) async-start(), calls=%async_computation.4 | async-start | bytes 8912896 | tf_op jit(solution)/shard_map/all_gather | solution.py:36
  274.7 203.4 %reduce-scatter.5.cloned.1.call-start = ((), (), s32[]{:S(2)}) async-start(), calls=%async_computation.5 | async-start | bytes 8912896 | tf_op jit(solution)/shard_map/reduce_scatter | solution.py:40
  375.9 1.3 copy-start.6
  375.9 102.2 %copy-start.3 = (bf16[128,2048]{1,0:T(8,128)(2,1)S(1)}, bf16[128,2048]{1,0:T(8,128)(2,1)}, u32[]{:S(2)}) copy-start(bf16[128,2048]{1,0:T(8,128)(2,1)} %param.6) | copy-start | bytes 1572868
  376.0 102.2 %copy-start.4 = (bf16[1,128,2048]{2,1,0:T(8,128)(2,1)S(1)}, bf16[1,128,2048]{2,1,0:T(8,128)(2,1)}, u32[]{:S(2)}) copy-start(bf16[1,128,2048]{2,1,0:T(8,128)(2,1)} %reduce-scatter.3.cloned.1.call-done) | copy-start | bytes 1572868
  376.0 114.6 %all-gather.12.cloned.1.call-start = ((), (), s32[]{:S(2)}) async-start(), calls=%async_computation.7 | async-start | bytes 4128768 | tf_op jit(solution)/shard_map/all_gather | solution.py:95
  378.8 185.2 %all-gather.10.cloned.1.call-start = ((), (), s32[]{:S(2)}) async-start(), calls=%async_computation.6 | async-start | bytes 8912896 | tf_op jit(solution)/shard_map/all_gather | solution.py:36
  479.4 14.7 %copy-start.5 = (bf16[128,2048]{1,0:T(8,128)(2,1)}, bf16[128,2048]{1,0:T(8,128)(2,1)S(1)}, u32[]{:S(2)}) copy-start(bf16[128,2048]{1,0:T(8,128)(2,1)S(1)} %fusion.26) | copy-start | bytes 1572868
  564.0 4.8 copy-start.2
  568.8 4.3 copy-start.1
Sparse Core Ops, SparseCore 0:
  11.0 77.6 all-gather.13
  173.2 101.4 reduce-scatter.2
  276.8 73.9 all-gather.7
  376.1 102.0 reduce-scatter.4
Sparse Core Ops, SparseCore 1:
  378.9 38.9 all-gather.11
  490.6 73.3 all-gather.9

commit v2 on v1

--- a/solution.py
+++ b/solution.py
@@ -1,6 +1,10 @@
+import functools
+
 import jax
 import jax.numpy as jnp
 from jax import lax
+from jax.experimental import pallas as pl
+from jax.experimental.pallas import tpu as pltpu
 from jax.sharding import PartitionSpec as P
 
 grad_scale = 0.03125
@@ -32,12 +36,299 @@
     return chosen.astype(jnp.bfloat16), slot_gate
 
 
-def gather_rows(rows):
-    return lax.all_gather(rows, "expert", axis=0, tiled=False)
+MESH = pl.DeviceIdType.MESH
+
+
+def ring_place(experts):
+    chips = experts // 2
+    side = chips // 2
+    me = lax.axis_index("expert")
+    core = me % 2
+    chip = me // 2
+    row, odd = chip // 2, chip % 2
+    place = row + odd * (chips - 1 - 2 * row)
+
+    def device(at):
+        at = (at + 2 * chips) % chips
+        back = at // side
+        return ((at + back * (chips - 1 - 2 * at)) * 2 + back) * 2
+
+    return place, core, device
+
+
+def ring_messages(chips):
+    side = chips // 2
+    return [
+        [(d, h) for d in range(1, side + 1) for h in range(2) if d < side or h == way]
+        for way in range(2)
+    ]
+
+
+def greet(peers):
+    barrier = pltpu.get_barrier_semaphore()
+    for peer in peers:
+        pl.semaphore_signal(barrier, inc=1, device_id={"expert": peer}, device_id_type=MESH)
+    pl.semaphore_wait(barrier, len(peers))
+
+
+def send(src, dst, send_sem, recv_sem, peer):
+    return pltpu.make_async_remote_copy(
+        src_ref=src,
+        dst_ref=dst,
+        send_sem=send_sem,
+        recv_sem=recv_sem,
+        device_id={"expert": peer},
+        device_id_type=MESH,
+    )
+
+
+def gather_kernel(experts, count, *refs):
+    mine, outs = refs[:count], refs[count : 2 * count]
+    hop_send, hop_recv, sib_send, sib_recv, own_sem, cross_sems = refs[2 * count :]
+    chips = experts // 2
+    messages = ring_messages(chips)
+    place, core, device = ring_place(experts)
+    me = lax.axis_index("expert")
+    sibling = me + 1 - 2 * core
+    peers = (device(place + 1) + core, device(place - 1) + core)
+    own = [pltpu.make_async_copy(mine[i], outs[i].at[me], own_sem.at[i]) for i in range(count)]
+    for copy in own:
+        copy.start()
+    greet(peers + (sibling,))
+
+    def rows_of(i, half):
+        size = mine[i].shape[0] // 2
+        return pl.ds(half * size, size)
+
+    def hop(i, way, index):
+        distance, half = messages[way][index]
+        sign = 1 - 2 * way
+        rows = rows_of(i, half)
+        origin = device(place - sign * (distance - 1)) + core
+        src = mine[i].at[rows] if distance == 1 else outs[i].at[origin, rows]
+        return send(
+            src,
+            outs[i].at[origin, rows],
+            hop_send.at[i, way, index],
+            hop_recv.at[i, way, index],
+            peers[way],
+        )
+
+    def landed(i, way, index, which):
+        distance, half = messages[way][index]
+        origin = device(place - (1 - 2 * way) * distance) + which
+        return outs[i].at[origin, rows_of(i, half)]
+
+    def across(i, way, index, which):
+        block = landed(i, way, index, which)
+        return send(
+            block, block, sib_send.at[i, way, index], sib_recv.at[i, way, index], sibling
+        )
+
+    for index in range(2):
+        for way in range(2):
+            for i in range(count):
+                if index < len(messages[way]) and messages[way][index][0] == 1:
+                    hop(i, way, index).start()
+    cross = [
+        send(mine[i], outs[i].at[me], cross_sems.at[0, i], cross_sems.at[1, i], sibling)
+        for i in range(count)
+    ]
+    for copy in cross:
+        copy.start()
+    for index in range(len(messages[0])):
+        for way in range(2):
+            distance, half = messages[way][index]
+            for i in range(count):
+                block = landed(i, way, index, core)
+                send(
+                    block,
+                    block,
+                    hop_send.at[i, way, index],
+                    hop_recv.at[i, way, index],
+                    peers[way],
+                ).wait_recv()
+                if (distance + 1, half) in messages[way]:
+                    hop(i, way, messages[way].index((distance + 1, half))).start()
+                across(i, way, index, core).start()
+    for i in range(count):
+        own[i].wait()
+        cross[i].wait_send()
+        send(
+            mine[i], outs[i].at[sibling], cross_sems.at[0, i], cross_sems.at[1, i], sibling
+        ).wait_recv()
+        for way in range(2):
+            for index in range(len(messages[way])):
+                hop(i, way, index).wait_send()
+                across(i, way, index, core).wait_send()
+                across(i, way, index, 1 - core).wait_recv()
+
+
+def gather_rows(arrays, name):
+    experts = lax.axis_size("expert")
+    count = len(arrays)
+    steps = len(ring_messages(experts // 2)[0])
+    dma = pltpu.SemaphoreType.DMA
+    return pl.pallas_call(
+        functools.partial(gather_kernel, experts, count),
+        out_shape=[jax.ShapeDtypeStruct((experts,) + a.shape, a.dtype) for a in arrays],
+        in_specs=[pl.BlockSpec(memory_space=pltpu.VMEM)] * count,
+        out_specs=[pl.BlockSpec(memory_space=pl.ANY)] * count,
+        scratch_shapes=[
+            dma((count, 2, steps)),
+            dma((count, 2, steps)),
+            dma((count, 2, steps)),
+            dma((count, 2, steps)),
+            dma((count,)),
+            dma((2, count)),
+        ],
+        compiler_params=pltpu.CompilerParams(
+            collective_id=name, has_side_effects=True, vmem_limit_bytes=8 * 1024 * 1024
+        ),
+        cost_estimate=pl.CostEstimate(
+            flops=20_000_000_000, bytes_accessed=20_000_000, transcendentals=0
+        ),
+        name="gather" + str(name),
+    )(*arrays)
+
+
+def scatter_kernel(
+    experts, parts, out, own, other, came, own_sem, sib_send, sib_recv, hop_send, hop_recv
+):
+    chips = experts // 2
+    side = chips // 2
+    messages = ring_messages(chips)
+    place, core, device = ring_place(experts)
+    me = lax.axis_index("expert")
+    sibling = me + 1 - 2 * core
+    peers = (device(place + 1) + core, device(place - 1) + core)
+    size = out.shape[0] // 2
+    order = [side]
+    for d in range(side - 1, 0, -1):
+        order += [d, chips - d]
+    order += [0]
+    loads = {
+        k: pltpu.make_async_copy(parts.at[device(place + k) + core], own.at[k], own_sem.at[k])
+        for k in order
+    }
+    for k in order:
+        loads[k].start()
+    greet(peers + (sibling,))
+    gifts = {
+        k: send(
+            parts.at[device(place + k) + 1 - core],
+            other.at[k],
+            sib_send.at[k],
+            sib_recv.at[k],
+            sibling,
+        )
+        for k in order
+    }
+    for k in order:
+        gifts[k].start()
+
+    def hop(way, message):
+        distance, half = message
+        k = distance if way == 0 else chips - distance
+        rows = pl.ds(half * size, size)
+        index = messages[way].index(message)
+        return send(
+            own.at[k, rows],
+            came.at[way, distance - 1, rows],
+            hop_send.at[way, index],
+            hop_recv.at[way, index],
+            peers[way],
+        )
+
+    step = 16
+
+    def add_up(k, half, more, target):
+        @pl.loop(0, size // step)
+        def _(at):
+            rows = pl.ds(pl.multiple_of(half * size + at * step, step), step)
+            total = own[k, rows, :].astype(jnp.float32) + other[k, rows, :].astype(jnp.float32)
+            for way, slot in more:
+                total = total + came[way, slot, rows, :].astype(jnp.float32)
+            if target is None:
+                own[k, rows, :] = total.astype(own.dtype)
+            else:
+                target[rows, :] = total.astype(target.dtype)
+
+    ready = set()
+
+    def get(k):
+        if k not in ready:
+            ready.add(k)
+            loads[k].wait()
+            gifts[k].wait_recv()
+
+    for distance in range(side, 0, -1):
+        for half in range(2):
+            for way in range(2):
+                if (distance, half) not in messages[way]:
+                    continue
+                k = distance if way == 0 else chips - distance
+                get(k)
+                more = []
+                if (distance + 1, half) in messages[way]:
+                    hop(way, (distance + 1, half)).wait_recv()
+                    more = [(way, distance)]
+                add_up(k, half, more, None)
+                hop(way, (distance, half)).start()
+    get(0)
+    for half in range(2):
+        more = []
+        for way in range(2):
+            if (1, half) in messages[way]:
+                hop(way, (1, half)).wait_recv()
+                more.append((way, 0))
+        add_up(0, half, more, out)
+    for k in order:
+        gifts[k].wait_send()
+    for way in range(2):
+        for message in messages[way]:
+            hop(way, message).wait_send()
 
 
 def scatter_sum(blocks):
-    return lax.psum_scatter(blocks, "expert", scatter_dimension=0, tiled=False)
+    experts, rows, width = blocks.shape
+    chips = experts // 2
+    steps = len(ring_messages(chips)[0])
+    dma = pltpu.SemaphoreType.DMA
+    buffers = (3 * chips + 4) * rows * width * 2
+    return pl.pallas_call(
+        functools.partial(scatter_kernel, experts),
+        out_shape=jax.ShapeDtypeStruct((rows, width), blocks.dtype),
+        in_specs=[pl.BlockSpec(memory_space=pl.ANY)],
+        out_specs=pl.BlockSpec(memory_space=pltpu.VMEM),
+        scratch_shapes=[
+            pltpu.VMEM((chips, rows, width), blocks.dtype),
+            pltpu.VMEM((chips, rows, width), blocks.dtype),
+            pltpu.VMEM((2, chips // 2, rows, width), blocks.dtype),
+            dma((chips,)),
+            dma((chips,)),
+            dma((chips,)),
+            dma((2, steps)),
+            dma((2, steps)),
+        ],
+        compiler_params=pltpu.CompilerParams(
+            collective_id=7, has_side_effects=True, vmem_limit_bytes=buffers + 2 * 1024 * 1024
+        ),
+        cost_estimate=pl.CostEstimate(
+            flops=20_000_000_000, bytes_accessed=20_000_000, transcendentals=0
+        ),
+        name="scatter_sum",
+    )(blocks)
+
+
+def from_groups(make):
+    groups = lax.axis_size("token")
+    mine = lax.axis_index("token")
+    taken = [make(mine)]
+    for shift in range(1, groups):
+        pairs = [(t, (t + shift) % groups) for t in range(groups)]
+        taken.append(lax.ppermute(make((mine + shift) % groups), "token", pairs))
+    return jnp.stack(taken)
 
 
 def pick(sel, rows):
@@ -46,9 +337,8 @@
     ).astype(jnp.bfloat16)
 
 
-def transpose_jacobian(token_rows, sel, slot_gate, slopes, up_weight, down_weight):
+def transpose_jacobian(everyone, sel, slot_gate, slopes, up_weight, down_weight):
     blocks, capacity, rows = sel.shape
-    everyone = gather_rows(token_rows)
     picked = pick(sel, everyone).reshape(blocks * capacity, -1)
     inner_prod = jnp.dot(picked, down_weight, preferred_element_type=jnp.float32)
     scaled = (inner_prod * slopes).astype(jnp.bfloat16)
@@ -68,31 +358,39 @@
 def body(cotangent, expert_ids, gate_values, hidden_pre, up_weight, down_weight):
     experts = lax.axis_size("expert")
     groups = lax.axis_size("token")
-    mine = lax.axis_index("token")
+    rows, width = cotangent.shape
+    top = expert_ids.shape[1]
+    padded = -(-2 * top // 16) * 16
+    routes = jnp.concatenate([expert_ids.T.astype(jnp.float32), gate_values.T], axis=0)
+    routes = jnp.pad(routes, ((0, padded - 2 * top), (0, 0)))
+    routes = from_groups(lambda group: routes).reshape(groups * padded, rows)
+    everyone, all_routes = gather_rows([cotangent, routes], 1)
     slopes, active = slope_and_act(hidden_pre[0])
     capacity = slopes.shape[0] // experts
-    both_ids = lax.all_gather(expert_ids, ("expert", "token"), axis=0, tiled=False)
-    both_gates = lax.all_gather(gate_values, ("expert", "token"), axis=0, tiled=False)
-    all_sel, all_gate = slot_tables(both_ids, both_gates, capacity)
-    all_sel = all_sel.reshape(experts, groups, capacity, -1)
-    all_gate = all_gate.reshape(experts, groups, capacity)
-    sel = lax.dynamic_index_in_dim(all_sel, mine, 1, keepdims=False)
-    slot_gate = lax.dynamic_index_in_dim(all_gate, mine, 1, keepdims=False)
+    acts = from_groups(lambda group: active)
+    all_routes = all_routes.reshape(experts * groups, padded, rows).transpose(0, 2, 1)
+    all_sel, all_gate = slot_tables(
+        all_routes[:, :, :top].astype(jnp.int32), all_routes[:, :, top : 2 * top], capacity
+    )
+    by_group = all_sel.reshape(experts, groups, capacity, rows)
+    sel = by_group[:, 0]
+    slot_gate = all_gate.reshape(experts, groups, capacity)[:, 0]
     first_term = transpose_jacobian(
-        cotangent, sel, slot_gate, slopes, up_weight[0], down_weight[0]
+        everyone, sel, slot_gate, slopes, up_weight[0], down_weight[0]
     )
-    second = transpose_jacobian(
-        first_term, sel, slot_gate, slopes, up_weight[0], down_weight[0]
-    )
+    (everyone,) = gather_rows([first_term], 2)
+    second = transpose_jacobian(everyone, sel, slot_gate, slopes, up_weight[0], down_weight[0])
     input_grad = (
         cotangent.astype(jnp.float32) + first_term.astype(jnp.float32) + second.astype(jnp.float32)
     ).astype(jnp.bfloat16)
-    rows = input_grad.shape[0]
-    columns = lax.all_to_all(input_grad, "token", split_axis=1, concat_axis=0, tiled=True)
-    everyone = gather_rows(columns).reshape(experts * groups, rows, -1)
-    picked = pick(all_sel.reshape(experts * groups, capacity, rows), everyone)
-    routed = (picked.astype(jnp.float32) * all_gate.reshape(-1, capacity, 1)).astype(jnp.bfloat16)
-    acts = lax.all_gather(active, "token", axis=0, tiled=False)
+    share = width // groups
+    columns = from_groups(
+        lambda group: lax.dynamic_slice_in_dim(input_grad, group * share, share, 1)
+    ).reshape(groups * rows, share)
+    (everyone,) = gather_rows([columns], 3)
+    everyone = everyone.reshape(experts * groups, rows, share)
+    picked = pick(all_sel, everyone)
+    routed = (picked.astype(jnp.float32) * all_gate[:, :, None]).astype(jnp.bfloat16)
     acts = acts.reshape(groups, experts, capacity, -1).transpose(1, 0, 2, 3)
     summed = lax.dot_general(
         routed.reshape(experts * groups * capacity, -1),

time: 581 us -> 302 us (0.52)
  waiting for transfers between devices: 347 us -> 5.3 us
  Pallas kernels: 0 us -> 233 us
  blocking collectives: 149 us -> 0 us
  between operations: 15.4 us -> 0.87 us
  matrix products: 59.4 us -> 45.9 us
    pallas_call x0 -> x5, Pallas kernels: none -> 233 us  [the longest x3 137 us: gather_rows(): pl.pallas_call(functools.partial(gather_kernel, experts, count), out_shap...]
    reduce_scatter x2 -> x0, waiting for transfers between devices: 201 us -> none  [scatter_sum(): return lax.psum_scatter(blocks, 'expert', scatter_dimension=0, tiled=False)]
    all_gather x4 -> x0, waiting for transfers between devices: 146 us -> none  [the longest x3 146 us: gather_rows(): return lax.all_gather(rows, 'expert', axis=0, tiled=False)]
    all_gather x2 -> x0, blocking collectives: 138 us -> none  [the longest x1 74 us: body(): lax.all_gather(expert_ids, ('expert', 'token'), axis=0, tiled=False)]
    all_to_all x1 -> x0, blocking collectives: 11 us -> none  [body(): lax.all_to_all(input_grad, 'token', split_axis=1, concat_axis=0, tiled=True)]
    dot_general x3, matrix products: 17.6 us -> 10.7 us  [pick(): lax.dot_general(sel, rows, (((2,), (1,)), ((0,), (0,))), preferred_elemen...]
    dot_general x2, matrix products: 15.5 us -> 8.87 us  [transpose_jacobian(): lax.dot_general(sel, weighted.reshape(blocks, capacity, -1), (((1,), (1,)...]
  transfers between devices with their start and end apart: 6 -> 3, of which waited for: 4 -> 1; matrix products, arithmetic and copies ran while one was open for 1% -> 15% of each run, Pallas kernels for 0% -> 77%
where the time goes in v2:
time: 302 us; the launch traced here: 301 us
  Pallas kernels  233 us (77%)
  matrix products  45.9 us (15%)
  other arithmetic  7.33 us (2%)
  waiting for transfers between devices  5.3 us (2%)
  starting transfers between devices  4.55 us (2%)
  local copies, waits for them, and re-layouts  4.46 us (1%)
    pallas_call x3, Pallas kernels, gather_rows(): pl.pallas_call(functools.partial(gather_kernel, experts, count), out_shap...  137 us
    pallas_call x2, Pallas kernels, scatter_sum(): pl.pallas_call(functools.partial(scatter_kernel, experts), out_shape=jax....  96.3 us
    dot_general x2, matrix products, transpose_jacobian(): lax.dot_general(scaled, up_weight, (((1,), (1,)), ((), ())), preferred_el...  22 us
    dot_general x3, matrix products, pick(): lax.dot_general(sel, rows, (((2,), (1,)), ((0,), (0,))), preferred_elemen...  10.7 us
    dot_general x2, matrix products, transpose_jacobian(): lax.dot_general(sel, weighted.reshape(blocks, capacity, -1), (((1,), (1,)...  8.87 us
  transfers between devices with their start and end apart: 3, of which 1 were waited for; matrix products, arithmetic and copies ran while one was open for 15% of the time, Pallas kernels for 77%

profile of v2, /device:TPU:0, one launch (start us, length us, event | category | flops | bytes accessed | tf_op | source)
XLA Modules:
  0.0 301.4 jit_solution(14363581898544157501)
XLA Ops:
  0.6 0.8 convert_bitcast_fusion.1
  1.5 0.8 fusion.48
  2.3 3.0 collective-permute-start
  5.3 2.6 fusion.17
  7.9 1.0 copy-done.3
  8.9 47.1 %gather1.1 = (bf16[16,128,2048]{2,1,0:T(8,128)(2,1)S(1)}, f32[16,32,128]{2,1,0:T(8,128)S(1)}) custom-call(bf16[128,2048]{1,0:T(8,128)(2,1)S(1)} %copy-done.3, f32[32,128]{1,0:T(8,128)S(1)} %bitcast.113), custom_call_target="tpu_custom_call" | custom-call | flops 20000000000 | bytes 20000000 | tf_op jit(solution)/shard_map/gather1/pallas_call | solution.py:172
  56.1 3.2 %copy-done.2 = bf16[16,128,2048]{2,1,0:T(8,128)(2,1)} copy-done((bf16[16,128,2048]{2,1,0:T(8,128)(2,1)}, bf16[16,128,2048]{2,1,0:T(8,128)(2,1)S(1)}, u32[]{:S(2)}) %copy-start.2) | copy-done | bytes 8388632
  59.6 0.4 select_reduce_fusion
  60.1 6.4 %convolution_convert_fusion.3 = bf16[16,56,2048]{2,1,0:T(8,128)(2,1)} fusion(bf16[16,128,2048]{2,1,0:T(8,128)(2,1)} %copy-done.2, s32[16,1,128]{2,0,1:T(8,128)S(1)} %copy.10), kind=kOutput, calls=%fused_computation.14 | convolution fusion | flops 471711744 | bytes 12066816 | tf_op jit(solution)/shard_map/dot_general | solution.py:335
  66.6 11.0 %multiply_convert_fusion.2 = bf16[896,2048]{1,0:T(8,128)(2,1)} fusion(f32[896]{0:T(1024)S(1)} %mul.99, bf16[1,2048,768]{2,1,0:T(8,128)(2,1)S(1)} %copy-done, bf16[896,2048]{1,0:T(8,128)(2,1)} %bitcast.115, bf16[1,2048,768]{2,1,0:T(8,128)(2,1)} %param.11, bf16[1,896,768]{2,1,0:T(8,128)(2,1)} %param.9), kind=kOutput, calls=%fused_computation.2 | convolution fusion | flops 5652054016 | bytes 15011328 | tf_op jit(solution)/shard_map/dot_general | solution.py:345
  77.5 4.4 %convolution_convert_fusion.1.parts = bf16[16,128,2048]{2,1,0:T(8,128)(2,1)S(1)} fusion(bf16[16,56,2048]{2,1,0:T(8,128)(2,1)} %bitcast.119, s32[16,1,128]{2,0,1:T(8,128)S(1)} %copy.10), kind=kOutput, calls=%fused_computation.4 | convolution fusion | flops 474071040 | bytes 12066816 | tf_op jit(solution)/shard_map/dot_general | solution.py:349
  82.0 48.7 %scatter_sum.2.refs_0_ = bf16[128,2048]{1,0:T(8,128)(2,1)S(1)} custom-call(bf16[16,128,2048]{2,1,0:T(8,128)(2,1)S(1)} %convolution_convert_fusion.1.parts), custom_call_target="tpu_custom_call" | custom-call | flops 20000000000 | bytes 20000000 | tf_op jit(solution)/shard_map/scatter_sum/pallas_call | solution.py:299
  130.7 44.9 %gather2.1 = bf16[16,128,2048]{2,1,0:T(8,128)(2,1)S(1)} custom-call(bf16[128,2048]{1,0:T(8,128)(2,1)S(1)} %scatter_sum.2.refs_0_), custom_call_target="tpu_custom_call" | custom-call | flops 20000000000 | bytes 20000000 | tf_op jit(solution)/shard_map/gather2/pallas_call | solution.py:172
  175.6 3.0 %convolution_convert_fusion.2 = bf16[16,56,2048]{2,1,0:T(8,128)(2,1)} fusion(bf16[16,128,2048]{2,1,0:T(8,128)(2,1)S(1)} %gather2.1, s32[16,1,128]{2,0,1:T(8,128)S(1)} %copy.10), kind=kOutput, calls=%fused_computation.13 | convolution fusion | flops 471711744 | bytes 12066816 | tf_op jit(solution)/shard_map/dot_general | solution.py:335
  178.6 11.0 %multiply_convert_fusion.1 = bf16[896,2048]{1,0:T(8,128)(2,1)} fusion(f32[896]{0:T(1024)S(1)} %mul.99, bf16[1,2048,768]{2,1,0:T(8,128)(2,1)S(1)} %copy-done, bf16[896,2048]{1,0:T(8,128)(2,1)} %bitcast.114, bf16[1,2048,768]{2,1,0:T(8,128)(2,1)} %param.11, bf16[1,896,768]{2,1,0:T(8,128)(2,1)} %param.9), kind=kOutput, calls=%fused_computation.1 | convolution fusion | flops 5652054016 | bytes 15011328 | tf_op jit(solution)/shard_map/dot_general | solution.py:345
  189.6 4.4 %convolution_convert_fusion.parts = bf16[16,128,2048]{2,1,0:T(8,128)(2,1)S(1)} fusion(bf16[16,56,2048]{2,1,0:T(8,128)(2,1)} %bitcast.118, s32[16,1,128]{2,0,1:T(8,128)S(1)} %copy.10), kind=kOutput, calls=%fused_computation.3 | convolution fusion | flops 474071040 | bytes 12066816 | tf_op jit(solution)/shard_map/dot_general | solution.py:349
  194.1 47.6 %scatter_sum.3 = bf16[128,2048]{1,0:T(8,128)(2,1)S(1)} custom-call(bf16[16,128,2048]{2,1,0:T(8,128)(2,1)S(1)} %convolution_convert_fusion.parts), custom_call_target="tpu_custom_call" | custom-call | flops 20000000000 | bytes 20000000 | tf_op jit(solution)/shard_map/scatter_sum/pallas_call | solution.py:299
  242.0 1.6 collective-permute-start.1
  243.6 0.7 fusion.21
  244.3 5.3 %collective-permute-done.1 = bf16[128,1024]{1,0:T(8,128)(2,1)S(1)} collective-permute-done((bf16[128,1024]{1,0:T(8,128)(2,1)S(1)}, bf16[128,1024]{1,0:T(8,128)(2,1)S(1)}, u32[]{:S(2)}, u32[]{:S(2)}) %collective-permute-start.1) | collective-permute-done | bytes 262176 | tf_op jit(solution)/shard_map/ppermute | solution.py:330
  249.6 44.6 %gather3.1 = bf16[16,256,1024]{2,1,0:T(8,128)(2,1)S(1)} custom-call(bf16[256,1024]{1,0:T(8,128)(2,1)S(1)} %bitcast.110), custom_call_target="tpu_custom_call" | custom-call | flops 20000000000 | bytes 20000000 | tf_op jit(solution)/shard_map/gather3/pallas_call | solution.py:172
  294.3 1.2 multiply_convert_fusion
  295.5 1.6 pad_maximum_fusion
  297.1 4.2 %fusion.26 = bf16[1,1024,768]{2,1,0:T(8,128)(2,1)} fusion(bf16[1792,1024]{1,0:T(8,128)(2,1)S(1)} %bitcast.117, bf16[1792,768]{1,0:T(8,128)(2,1)S(1)} %bitcast.120), kind=kOutput, calls=%fused_computation.36 | convolution fusion | flops 2820145152 | bytes 7995392 | tf_op jit(solution)/shard_map/dot_general | solution.py:395
  (30 shorter events, 0.8 us)
Async XLA Ops:
  0.6 65.9 %copy-start = (bf16[1,2048,768]{2,1,0:T(8,128)(2,1)S(1)}, bf16[1,2048,768]{2,1,0:T(8,128)(2,1)}, u32[]{:S(2)}) copy-start(bf16[1,2048,768]{2,1,0:T(8,128)(2,1)} %param.10) | copy-start | bytes 9437188
  2.3 5.6 %collective-permute-start = (f32[16,128]{1,0:T(8,128)S(1)}, f32[16,128]{1,0:T(8,128)S(1)}, u32[]{:S(2)}, u32[]{:S(2)}) collective-permute-start(f32[16,128]{1,0:T(8,128)S(1)} %get-tuple-element.11), channel_id=1, source_target_pairs={{0,1},{1,0},{2,3},{3,2},{4,5},{5,4},{6,7},{7,6},{8,9},{9,8},{10,11... | collective-permute-start | bytes 24584 | tf_op jit(solution)/shard_map/ppermute | solution.py:330
  7.9 287.6 %collective-permute-start.2 = (bf16[896,768]{1,0:T(8,128)(2,1)}, bf16[896,768]{1,0:T(8,128)(2,1)}, u32[]{:S(2)}, u32[]{:S(2)}) collective-permute-start(bf16[896,768]{1,0:T(8,128)(2,1)} %fusion.17), channel_id=1, source_target_pairs={{0,1},{1,0},{2,3},{3,2},{4,5},{5,4},{6,7},{7,6},{8,9},{9,8},{10,11... | collective-permute-start | bytes 4128776 | tf_op jit(solution)/shard_map/ppermute | solution.py:330
  7.9 1.0 copy-start.3
  56.1 3.2 %copy-start.2 = (bf16[16,128,2048]{2,1,0:T(8,128)(2,1)}, bf16[16,128,2048]{2,1,0:T(8,128)(2,1)S(1)}, u32[]{:S(2)}) copy-start(bf16[16,128,2048]{2,1,0:T(8,128)(2,1)S(1)} %get-tuple-element.5) | copy-start | bytes 25165828
  130.7 44.9 %copy-start.5 = (bf16[128,2048]{1,0:T(8,128)(2,1)}, bf16[128,2048]{1,0:T(8,128)(2,1)S(1)}, u32[]{:S(2)}) copy-start(bf16[128,2048]{1,0:T(8,128)(2,1)S(1)} %scatter_sum.2.refs_0_) | copy-start | bytes 1572868
  194.0 47.6 %copy-start.4 = (bf16[128,2048]{1,0:T(8,128)(2,1)S(1)}, bf16[128,2048]{1,0:T(8,128)(2,1)}, u32[]{:S(2)}) copy-start(bf16[128,2048]{1,0:T(8,128)(2,1)} %refs_0_.1) | copy-start | bytes 1572868
  194.1 47.6 %copy-start.6 = (bf16[128,2048]{1,0:T(8,128)(2,1)S(1)}, bf16[128,2048]{1,0:T(8,128)(2,1)}, u32[]{:S(2)}) copy-start(bf16[128,2048]{1,0:T(8,128)(2,1)} %copy-done.5) | copy-start | bytes 1572868
  241.7 1.9 copy-start.7
  241.9 52.3 %copy-start.8 = (bf16[128,2048]{1,0:T(8,128)(2,1)}, bf16[128,2048]{1,0:T(8,128)(2,1)S(1)}, u32[]{:S(2)}) copy-start(bf16[128,2048]{1,0:T(8,128)(2,1)S(1)} %add_convert_fusion) | copy-start | bytes 1572868
  242.0 7.5 %collective-permute-start.1 = (bf16[128,1024]{1,0:T(8,128)(2,1)S(1)}, bf16[128,1024]{1,0:T(8,128)(2,1)S(1)}, u32[]{:S(2)}, u32[]{:S(2)}) collective-permute-start(bf16[128,1024]{1,0:T(8,128)(2,1)S(1)} %get-tuple-element.9), channel_id=1, source_target_pairs={{0,1},{1,0},{2,3},{3,2},{4,5},{5,4},{6,7},{7,6},{8,9},{9,8},{10,11... | collective-permute-start | bytes 786440 | tf_op jit(solution)/shard_map/ppermute | solution.py:330
  297.1 4.3 %copy-start.1 = (bf16[1,2048,768]{2,1,0:T(8,128)(2,1)S(1)}, bf16[1,2048,768]{2,1,0:T(8,128)(2,1)}, u32[]{:S(2)}) copy-start(bf16[1,2048,768]{2,1,0:T(8,128)(2,1)} %param.10) | copy-start | bytes 9437188

commit v3 on v2

--- a/solution.py
+++ b/solution.py
@@ -83,8 +83,10 @@
 
 
 def gather_kernel(experts, count, *refs):
-    mine, outs = refs[:count], refs[count : 2 * count]
-    hop_send, hop_recv, sib_send, sib_recv, own_sem, cross_sems = refs[2 * count :]
+    hop_send, hop_recv, sib_send, sib_recv, own_sem, cross_sems = refs[-6:]
+    mine, refs = refs[:count], refs[count:-6]
+    hidden = refs[: (len(refs) - count) // 3]
+    outs = refs[len(hidden) : len(hidden) + count]
     chips = experts // 2
     messages = ring_messages(chips)
     place, core, device = ring_place(experts)
@@ -136,6 +138,15 @@
     ]
     for copy in cross:
         copy.start()
+    if hidden:
+        (hidden_ref,), (slope_ref, act_ref) = hidden, refs[1 + count :]
+        step = 16
+
+        @pl.loop(0, hidden_ref.shape[0] // step)
+        def _(at):
+            rows = pl.ds(pl.multiple_of(at * step, step), step)
+            slope_ref[rows, :], act_ref[rows, :] = slope_and_act(hidden_ref[rows, :])
+
     for index in range(len(messages[0])):
         for way in range(2):
             distance, half = messages[way][index]
@@ -164,16 +175,18 @@
                 across(i, way, index, 1 - core).wait_recv()
 
 
-def gather_rows(arrays, name):
+def gather_rows(arrays, name, hidden=()):
     experts = lax.axis_size("expert")
     count = len(arrays)
     steps = len(ring_messages(experts // 2)[0])
     dma = pltpu.SemaphoreType.DMA
     return pl.pallas_call(
         functools.partial(gather_kernel, experts, count),
-        out_shape=[jax.ShapeDtypeStruct((experts,) + a.shape, a.dtype) for a in arrays],
-        in_specs=[pl.BlockSpec(memory_space=pltpu.VMEM)] * count,
-        out_specs=[pl.BlockSpec(memory_space=pl.ANY)] * count,
+        out_shape=[jax.ShapeDtypeStruct((experts,) + a.shape, a.dtype) for a in arrays]
+        + [jax.ShapeDtypeStruct(a.shape, kind) for a in hidden for kind in (jnp.float32, a.dtype)],
+        in_specs=[pl.BlockSpec(memory_space=pltpu.VMEM)] * (count + len(hidden)),
+        out_specs=[pl.BlockSpec(memory_space=pl.ANY)] * count
+        + [pl.BlockSpec(memory_space=pltpu.VMEM)] * (2 * len(hidden)),
         scratch_shapes=[
             dma((count, 2, steps)),
             dma((count, 2, steps)),
@@ -183,13 +196,13 @@
             dma((2, count)),
         ],
         compiler_params=pltpu.CompilerParams(
-            collective_id=name, has_side_effects=True, vmem_limit_bytes=8 * 1024 * 1024
+            collective_id=name, has_side_effects=True, vmem_limit_bytes=(16 if hidden else 8) * 1024 * 1024
         ),
         cost_estimate=pl.CostEstimate(
             flops=20_000_000_000, bytes_accessed=20_000_000, transcendentals=0
         ),
         name="gather" + str(name),
-    )(*arrays)
+    )(*arrays, *hidden)
 
 
 def scatter_kernel(
@@ -364,8 +377,7 @@
     routes = jnp.concatenate([expert_ids.T.astype(jnp.float32), gate_values.T], axis=0)
     routes = jnp.pad(routes, ((0, padded - 2 * top), (0, 0)))
     routes = from_groups(lambda group: routes).reshape(groups * padded, rows)
-    everyone, all_routes = gather_rows([cotangent, routes], 1)
-    slopes, active = slope_and_act(hidden_pre[0])
+    everyone, all_routes, slopes, active = gather_rows([cotangent, routes], 1, [hidden_pre[0]])
     capacity = slopes.shape[0] // experts
     acts = from_groups(lambda group: active)
     all_routes = all_routes.reshape(experts * groups, padded, rows).transpose(0, 2, 1)

time: 302 us -> 305 us (level)
  other arithmetic: 7.33 us -> 2.74 us
  local copies, waits for them, and re-layouts: 4.46 us -> 8.45 us
  waiting for transfers between devices: 5.3 us -> 8.78 us
    unnamed x19 -> x25, local copies, waits for them, and re-layouts: 4.3 us -> 8.29 us
    ppermute x3, waiting for transfers between devices: 5.3 us -> 8.78 us  [from_groups(): taken.append(lax.ppermute(make((mine + shift) % groups), 'token', pairs))]
    convert_element_type x2 -> x0, other arithmetic: 3.27 us -> none  [slope_and_act(): active = (values * normal_cdf).astype(jnp.bfloat16)]
  transfers between devices with their start and end apart: 3 -> 3, of which waited for: 1 -> 2; matrix products, arithmetic and copies ran while one was open for 15% -> 0% of each run, Pallas kernels for 77% -> 15%
where the time goes in v3:
time: 305 us
  Pallas kernels  233 us (76%)
  matrix products  46.2 us (15%)
  waiting for transfers between devices  8.78 us (3%)
  local copies, waits for them, and re-layouts  8.45 us (3%)
  starting transfers between devices  5.06 us (2%)
    pallas_call x3, Pallas kernels, gather_rows(): pl.pallas_call(functools.partial(gather_kernel, experts, count), out_shap...  137 us
    pallas_call x2, Pallas kernels, scatter_sum(): pl.pallas_call(functools.partial(scatter_kernel, experts), out_shape=jax....  96.3 us
    dot_general x2, matrix products, transpose_jacobian(): lax.dot_general(scaled, up_weight, (((1,), (1,)), ((), ())), preferred_el...  22.3 us
    dot_general x3, matrix products, pick(): lax.dot_general(sel, rows, (((2,), (1,)), ((0,), (0,))), preferred_elemen...  10.7 us
    dot_general x2, matrix products, transpose_jacobian(): lax.dot_general(sel, weighted.reshape(blocks, capacity, -1), (((1,), (1,)...  8.87 us
    ppermute x3, waiting for transfers between devices, from_groups(): taken.append(lax.ppermute(make((mine + shift) % groups), 'token', pairs))  8.78 us
    unnamed x25, local copies, waits for them, and re-layouts  8.29 us
  transfers between devices with their start and end apart: 3, of which 2 were waited for; matrix products, arithmetic and copies ran while one was open for 0% of the time, Pallas kernels for 15%

profile of v3, /device:TPU:0, one launch (start us, length us, event | category | flops | bytes accessed | tf_op | source)
XLA Modules:
  0.0 305.0 jit_solution(14514980199463143209)
XLA Ops:
  0.6 0.8 convert_bitcast_fusion
  1.5 0.8 fusion.28
  2.3 3.0 collective-permute-start
  5.3 1.6 collective-permute-done
  6.9 1.0 copy-done.5
  7.9 1.3 copy-done.9
  9.3 47.1 %gather1.1 = (bf16[16,128,2048]{2,1,0:T(8,128)(2,1)S(1)}, f32[16,32,128]{2,1,0:T(8,128)S(1)}, f32[896,768]{1,0:T(8,128)S(1)}, bf16[896,768]{1,0:T(8,128)(2,1)S(1)}) custom-call(bf16[128,2048]{1,0:T(8,128)(2,1)S(1)} %copy-done.5, f32[32,128]{1,0:T(8,128)S(1)} %bitcast.73, bf16[896,768]{1,0:T(8,128)(2,1)S(1)} %bitcast.74), custom_call_target="tpu_custom_call" | custom-call | flops 20000000000 | bytes 20000000 | tf_op jit(solution)/shard_map/gather1/pallas_call | solution.py:183
  56.4 3.2 %copy-done.2 = bf16[16,128,2048]{2,1,0:T(8,128)(2,1)} copy-done((bf16[16,128,2048]{2,1,0:T(8,128)(2,1)}, bf16[16,128,2048]{2,1,0:T(8,128)(2,1)S(1)}, u32[]{:S(2)}) %copy-start.2) | copy-done | bytes 8388632
  59.7 1.1 copy-done.3
  60.7 1.6 copy-done.10
  63.1 6.4 %convolution_convert_fusion.3 = bf16[16,56,2048]{2,1,0:T(8,128)(2,1)} fusion(bf16[16,128,2048]{2,1,0:T(8,128)(2,1)} %copy-done.2, s32[16,1,128]{2,0,1:T(8,128)S(1)} %copy.12), kind=kOutput, calls=%fused_computation.6 | convolution fusion | flops 471711744 | bytes 12066816 | tf_op jit(solution)/shard_map/dot_general | solution.py:348
  69.6 11.1 %multiply_convert_fusion.2 = bf16[896,2048]{1,0:T(8,128)(2,1)} fusion(f32[896]{0:T(1024)S(1)} %mul.43, bf16[1,2048,768]{2,1,0:T(8,128)(2,1)S(1)} %copy-done, f32[896,768]{1,0:T(8,128)} %copy-done.10, bf16[896,2048]{1,0:T(8,128)(2,1)} %bitcast.76, bf16[1,2048,768]{2,1,0:T(8,128)(2,1)} %param.11), kind=kOutput, calls=%fused_computation.2 | convolution fusion | flops 5645860864 | bytes 16387584 | tf_op jit(solution)/shard_map/dot_general | solution.py:358
  80.7 4.4 %convolution_convert_fusion.1.parts = bf16[16,128,2048]{2,1,0:T(8,128)(2,1)S(1)} fusion(bf16[16,56,2048]{2,1,0:T(8,128)(2,1)} %bitcast.79, s32[16,1,128]{2,0,1:T(8,128)S(1)} %copy.12), kind=kOutput, calls=%fused_computation.4 | convolution fusion | flops 474071040 | bytes 12066816 | tf_op jit(solution)/shard_map/dot_general | solution.py:362
  85.1 48.7 %scatter_sum.2.refs_0_ = bf16[128,2048]{1,0:T(8,128)(2,1)S(1)} custom-call(bf16[16,128,2048]{2,1,0:T(8,128)(2,1)S(1)} %convolution_convert_fusion.1.parts), custom_call_target="tpu_custom_call" | custom-call | flops 20000000000 | bytes 20000000 | tf_op jit(solution)/shard_map/scatter_sum/pallas_call | solution.py:312
  133.8 44.9 %gather2.1 = bf16[16,128,2048]{2,1,0:T(8,128)(2,1)S(1)} custom-call(bf16[128,2048]{1,0:T(8,128)(2,1)S(1)} %scatter_sum.2.refs_0_), custom_call_target="tpu_custom_call" | custom-call | flops 20000000000 | bytes 20000000 | tf_op jit(solution)/shard_map/gather2/pallas_call | solution.py:183
  178.7 3.0 convolution_convert_fusion.2
  181.8 11.1 %multiply_convert_fusion.1 = bf16[896,2048]{1,0:T(8,128)(2,1)} fusion(f32[896]{0:T(1024)S(1)} %mul.43, bf16[1,2048,768]{2,1,0:T(8,128)(2,1)S(1)} %copy-done, f32[896,768]{1,0:T(8,128)} %copy-done.10, bf16[896,2048]{1,0:T(8,128)(2,1)} %bitcast.75, bf16[1,2048,768]{2,1,0:T(8,128)(2,1)} %param.11), kind=kOutput, calls=%fused_computation.1 | convolution fusion | flops 5645860864 | bytes 16387584 | tf_op jit(solution)/shard_map/dot_general | solution.py:358
  192.9 4.4 %convolution_convert_fusion.parts = bf16[16,128,2048]{2,1,0:T(8,128)(2,1)S(1)} fusion(bf16[16,56,2048]{2,1,0:T(8,128)(2,1)} %bitcast.78, s32[16,1,128]{2,0,1:T(8,128)S(1)} %copy.12), kind=kOutput, calls=%fused_computation.3 | convolution fusion | flops 474071040 | bytes 12066816 | tf_op jit(solution)/shard_map/dot_general | solution.py:362
  197.4 47.6 %scatter_sum.3 = bf16[128,2048]{1,0:T(8,128)(2,1)S(1)} custom-call(bf16[16,128,2048]{2,1,0:T(8,128)(2,1)S(1)} %convolution_convert_fusion.parts), custom_call_target="tpu_custom_call" | custom-call | flops 20000000000 | bytes 20000000 | tf_op jit(solution)/shard_map/scatter_sum/pallas_call | solution.py:312
  245.3 1.6 collective-permute-start.1
  247.4 7.1 %collective-permute-done.1 = bf16[128,1024]{1,0:T(8,128)(2,1)S(1)} collective-permute-done((bf16[128,1024]{1,0:T(8,128)(2,1)S(1)}, bf16[128,1024]{1,0:T(8,128)(2,1)S(1)}, u32[]{:S(2)}, u32[]{:S(2)}) %collective-permute-start.1) | collective-permute-done | bytes 262176 | tf_op jit(solution)/shard_map/ppermute | solution.py:343
  254.6 44.6 %gather3.1 = bf16[16,256,1024]{2,1,0:T(8,128)(2,1)S(1)} custom-call(bf16[256,1024]{1,0:T(8,128)(2,1)S(1)} %bitcast.70), custom_call_target="tpu_custom_call" | custom-call | flops 20000000000 | bytes 20000000 | tf_op jit(solution)/shard_map/gather3/pallas_call | solution.py:183
  299.2 1.2 multiply_convert_fusion
  300.7 4.2 %fusion.10 = bf16[1,1024,768]{2,1,0:T(8,128)(2,1)} fusion(bf16[1792,1024]{1,0:T(8,128)(2,1)S(1)} %bitcast.77, bf16[1792,768]{1,0:T(8,128)(2,1)S(1)} %bitcast.80), kind=kOutput, calls=%fused_computation.17 | convolution fusion | flops 2820145152 | bytes 7995392 | tf_op jit(solution)/shard_map/dot_general | solution.py:407
  (34 shorter events, 1.9 us)
Async XLA Ops:
  0.6 68.9 %copy-start = (bf16[1,2048,768]{2,1,0:T(8,128)(2,1)S(1)}, bf16[1,2048,768]{2,1,0:T(8,128)(2,1)}, u32[]{:S(2)}) copy-start(bf16[1,2048,768]{2,1,0:T(8,128)(2,1)} %param.10) | copy-start | bytes 9437188
  2.3 4.6 %collective-permute-start = (f32[16,128]{1,0:T(8,128)S(1)}, f32[16,128]{1,0:T(8,128)S(1)}, u32[]{:S(2)}, u32[]{:S(2)}) collective-permute-start(f32[16,128]{1,0:T(8,128)S(1)} %get-tuple-element.15), channel_id=1, source_target_pairs={{0,1},{1,0},{2,3},{3,2},{4,5},{5,4},{6,7},{7,6},{8,9},{9,8},{10,11... | collective-permute-start | bytes 24584 | tf_op jit(solution)/shard_map/ppermute | solution.py:343
  6.9 1.0 copy-start.5
  7.9 1.3 copy-start.9
  56.4 3.2 %copy-start.2 = (bf16[16,128,2048]{2,1,0:T(8,128)(2,1)}, bf16[16,128,2048]{2,1,0:T(8,128)(2,1)S(1)}, u32[]{:S(2)}) copy-start(bf16[16,128,2048]{2,1,0:T(8,128)(2,1)S(1)} %get-tuple-element.7) | copy-start | bytes 25165828
  59.7 1.1 copy-start.3
  60.7 1.6 copy-start.10
  133.8 44.9 %copy-start.7 = (bf16[128,2048]{1,0:T(8,128)(2,1)}, bf16[128,2048]{1,0:T(8,128)(2,1)S(1)}, u32[]{:S(2)}) copy-start(bf16[128,2048]{1,0:T(8,128)(2,1)S(1)} %scatter_sum.2.refs_0_) | copy-start | bytes 1572868
  197.4 47.6 %copy-start.6 = (bf16[128,2048]{1,0:T(8,128)(2,1)S(1)}, bf16[128,2048]{1,0:T(8,128)(2,1)}, u32[]{:S(2)}) copy-start(bf16[128,2048]{1,0:T(8,128)(2,1)} %refs_0_.1) | copy-start | bytes 1572868
  197.4 47.6 %copy-start.8 = (bf16[128,2048]{1,0:T(8,128)(2,1)S(1)}, bf16[128,2048]{1,0:T(8,128)(2,1)}, u32[]{:S(2)}) copy-start(bf16[128,2048]{1,0:T(8,128)(2,1)} %copy-done.7) | copy-start | bytes 1572868
  197.4 49.5 %copy-start.4 = (bf16[896,768]{1,0:T(8,128)(2,1)S(1)}, bf16[896,768]{1,0:T(8,128)(2,1)}, u32[]{:S(2)}) copy-start(bf16[896,768]{1,0:T(8,128)(2,1)} %copy-done.3) | copy-start | bytes 4128772
  245.2 54.0 %copy-start.11 = (bf16[128,2048]{1,0:T(8,128)(2,1)}, bf16[128,2048]{1,0:T(8,128)(2,1)S(1)}, u32[]{:S(2)}) copy-start(bf16[128,2048]{1,0:T(8,128)(2,1)S(1)} %add_convert_fusion) | copy-start | bytes 1572868
  245.3 9.2 %collective-permute-start.1 = (bf16[128,1024]{1,0:T(8,128)(2,1)S(1)}, bf16[128,1024]{1,0:T(8,128)(2,1)S(1)}, u32[]{:S(2)}, u32[]{:S(2)}) collective-permute-start(bf16[128,1024]{1,0:T(8,128)(2,1)S(1)} %get-tuple-element.13), channel_id=1, source_target_pairs={{0,1},{1,0},{2,3},{3,2},{4,5},{5,4},{6,7},{7,6},{8,9},{9,8},{10,11... | collective-permute-start | bytes 786440 | tf_op jit(solution)/shard_map/ppermute | solution.py:343
  246.9 53.6 %collective-permute-start.2 = (bf16[896,768]{1,0:T(8,128)(2,1)S(1)}, bf16[896,768]{1,0:T(8,128)(2,1)S(1)}, u32[]{:S(2)}, u32[]{:S(2)}) collective-permute-start(bf16[896,768]{1,0:T(8,128)(2,1)S(1)} %copy-done.4), channel_id=1, source_target_pairs={{0,1},{1,0},{2,3},{3,2},{4,5},{5,4},{6,7},{7,6},{8,9},{9,8},{10,11... | collective-permute-start | bytes 4128776 | tf_op jit(solution)/shard_map/ppermute | solution.py:343
  300.7 4.3 %copy-start.1 = (bf16[1,2048,768]{2,1,0:T(8,128)(2,1)S(1)}, bf16[1,2048,768]{2,1,0:T(8,128)(2,1)}, u32[]{:S(2)}) copy-start(bf16[1,2048,768]{2,1,0:T(8,128)(2,1)} %param.10) | copy-start | bytes 9437188
